TPU v7x, 32 devices: a whole 2x2x4 slice. The times are simulated.
32 devices in a mesh: row: 8 (over z, y), col: 4 (over x, core).
Axes of the slice: x: 2, y: 2, z: 4, core: 2. Of those that a mesh axis runs over, the one named last changes fastest.
Arguments:
- root_rhs: bfloat16 [8, 8192], replicated, may hold values from -6 to 6
- diag_inv: bfloat16 [16, 512, 512], replicated, may hold values from -1 to 2
- tile_u: bfloat16 [8, 4, 2, 4, 128, 512], P('row', 'col'), may hold values from -0.1875 to 0.1875
- tile_v: bfloat16 [8, 4, 2, 4, 512, 128], P('row', 'col'), may hold values from -0.25 to 0.25
- tile_rank: int32 [8, 4, 2, 4], P('row', 'col'), may hold values from 16 to 128
- child_x: bfloat16 [32, 8, 512], P(('row', 'col')), may hold values from -6 to 6
- border_t: bfloat16 [32, 512, 1024], P(('row', 'col')), may hold values from -0.09375 to 0.09375
- child_inv: bfloat16 [32, 512, 512], P(('row', 'col')), may hold values from -1 to 2
- child_blocks: int32 [32, 8], P(('row', 'col')), may hold values from 0 to 63
Outputs:
- root_solution: float32 [8, 8192], P(None, ('row', 'col'))
- child_out: float32 [32, 8, 512], P(('row', 'col'))
All inputs are finite; a program needn't handle non-finite values.
Results may differ from a plain program's by a relative error of at most 0.017.
Values sent between devices are 32-bit elements; how exact they have to be, the bound alone decides.
A program may use at most 64 MiB of HBM per device.

v0:
```python
import jax
import jax.numpy as jnp
from jax import lax
from jax.sharding import PartitionSpec as P

BLK = 128
BB = 8


def per_device(
    root_rhs, diag_inv, tile_u, tile_v, tile_rank, child_x, border_t, child_inv, child_blocks
):
    highest_precision = lax.Precision.HIGHEST
    n_row = lax.axis_size("row")
    n_col = lax.axis_size("col")
    my_row = lax.axis_index("row")
    my_col = lax.axis_index("col")
    ntile = diag_inv.shape[0]
    tile = diag_inv.shape[1]
    rhs_count = root_rhs.shape[0]
    rank_max = tile_u.shape[4]
    t_rows = tile_u.shape[2]
    t_cols = tile_u.shape[3]
    left_tiles = tile_u[0, 0]
    right_tiles = tile_v[0, 0]
    tile_ranks = tile_rank[0, 0]
    blocks_per_front = tile // BLK
    n_child = child_x.shape[0]
    upward = jnp.einsum("crs,csb->crb", child_x, border_t, preferred_element_type=jnp.float32)
    pieces = (
        upward.reshape(n_child, rhs_count, BB, BLK)
        .transpose(1, 0, 2, 3)
        .reshape(rhs_count, n_child * BB, BLK)
    )
    flat_blocks = child_blocks.reshape(-1)
    dense_sum = (
        jnp.zeros((rhs_count, ntile * blocks_per_front, BLK), jnp.float32)
        .at[:, flat_blocks, :]
        .add(pieces)
    )
    dense_sum = dense_sum.reshape(rhs_count, ntile, tile)
    right_side = root_rhs.reshape(rhs_count, ntile, tile)
    col_ids = my_col + n_col * jnp.arange(t_cols)
    row_ids = my_row + n_row * jnp.arange(t_rows)
    rank_iota = jnp.arange(rank_max)

    def forward(column, solved_rows):
        owner_slot = column // n_row
        on_row = column % n_row == my_row
        known_cols = jnp.take(solved_rows, col_ids, axis=1).astype(jnp.bfloat16)
        right_row = lax.dynamic_index_in_dim(right_tiles, owner_slot, 0, keepdims=False)
        left_row_index = lax.dynamic_index_in_dim(left_tiles, owner_slot, 0, keepdims=False)
        rank_row = lax.dynamic_index_in_dim(tile_ranks, owner_slot, 0, keepdims=False)
        live_mask = (rank_iota[None, :] < rank_row[:, None]) & (col_ids[:, None] < column) & on_row
        coefficient_values = jnp.einsum(
            "rbt,btq->rbq", known_cols, right_row, preferred_element_type=jnp.float32
        )
        coefficient_values = jnp.where(live_mask[None], coefficient_values, 0.0).astype(
            jnp.bfloat16
        )
        partial_value = jnp.einsum(
            "rbq,bqt->rt", coefficient_values, left_row_index, preferred_element_type=jnp.float32
        )
        carried = lax.dynamic_index_in_dim(dense_sum, column, 1, keepdims=False)
        row_total = lax.psum(partial_value + carried, ("row", "col"))
        block_rhs = lax.dynamic_index_in_dim(right_side, column, 1, keepdims=False).astype(
            jnp.float32
        )
        inverse = lax.dynamic_index_in_dim(diag_inv, column, 0, keepdims=False).astype(jnp.float32)
        fresh = jnp.dot(block_rhs - row_total, inverse, precision=highest_precision)
        return lax.dynamic_update_index_in_dim(solved_rows, fresh, column, 1)

    solved_rows = lax.fori_loop(0, ntile, forward, jnp.zeros((rhs_count, ntile, tile), jnp.float32))

    def backward(sweep, result):
        column = ntile - 1 - sweep
        owner_slot = column // n_col
        on_col = column % n_col == my_col
        known_rows = jnp.take(result, row_ids, axis=1).astype(jnp.bfloat16)
        left_col = lax.dynamic_index_in_dim(left_tiles, owner_slot, 1, keepdims=False)
        right_col = lax.dynamic_index_in_dim(right_tiles, owner_slot, 1, keepdims=False)
        rank_col = lax.dynamic_index_in_dim(tile_ranks, owner_slot, 1, keepdims=False)
        live_mask = (rank_iota[None, :] < rank_col[:, None]) & (row_ids[:, None] > column) & on_col
        coefficient_values = jnp.einsum(
            "rat,aqt->raq", known_rows, left_col, preferred_element_type=jnp.float32
        )
        coefficient_values = jnp.where(live_mask[None], coefficient_values, 0.0).astype(
            jnp.bfloat16
        )
        partial_value = jnp.einsum(
            "raq,atq->rt", coefficient_values, right_col, preferred_element_type=jnp.float32
        )
        col_total = lax.psum(partial_value, ("row", "col"))
        block_solved = lax.dynamic_index_in_dim(solved_rows, column, 1, keepdims=False)
        inverse = lax.dynamic_index_in_dim(diag_inv, column, 0, keepdims=False).astype(jnp.float32)
        fresh = jnp.dot(block_solved - col_total, inverse.T, precision=highest_precision)
        return lax.dynamic_update_index_in_dim(result, fresh, column, 1)

    result = lax.fori_loop(0, ntile, backward, jnp.zeros((rhs_count, ntile, tile), jnp.float32))
    share = ntile * tile // (n_row * n_col)
    start = (my_row * n_col + my_col) * share
    root_part = lax.dynamic_slice_in_dim(result.reshape(rhs_count, ntile * tile), start, share, 1)
    gathered = result.reshape(rhs_count, ntile * blocks_per_front, BLK)[:, flat_blocks, :]
    gathered = gathered.reshape(rhs_count, n_child, BB * BLK).astype(jnp.bfloat16)
    returned = jnp.einsum("rcb,csb->crs", gathered, border_t, preferred_element_type=jnp.float32)
    child_out = child_x.astype(jnp.float32) - jnp.einsum(
        "crs,cst->crt", returned, child_inv.astype(jnp.float32), precision=highest_precision
    )
    return (root_part, child_out)


def solution(mesh):
    return jax.shard_map(
        per_device,
        mesh=mesh,
        in_specs=(
            P(),
            P(),
            P("row", "col", None, None, None, None),
            P("row", "col", None, None, None, None),
            P("row", "col", None, None),
            P(("row", "col"), None, None),
            P(("row", "col"), None, None),
            P(("row", "col"), None, None),
            P(("row", "col"), None),
        ),
        out_specs=(P(None, ("row", "col")), P(("row", "col"), None, None)),
        check_vma=False,
    )
```

profile of v0, /device:TPU:0, one launch (start us, length us, event | category | flops | bytes accessed | tf_op | source)
XLA Modules:
  0.0 1424.4 jit_solution(4886888711580385367)
XLA Ops:
  5.8 715.2 %while.32 = (s32[]{:T(128)}, f32[8,16,512]{2,0,1:T(8,128)S(1)}, bf16[8,16,512]{2,1,0:T(8,128)(2,1)S(1)}, s32[2,4]{1,0:T(2,128)}, s32[]{:T(128)}, /*index=5*/bf16...) while((s32[]{:T(128)}, f32[8,16,512]{2,0,1:T(8,128)S(1)}, ...), condition=%wide.region_3.4_spmd.clone, body=%wide.region_1.3_spmd.clone.sunk | while | flops 33598024 | bytes 1818560 | solution.py:73
  7.2 1.8 fusion.106
  9.0 42.0 %psum.32 = f32[8,512]{1,0:T(8,128)S(1)} all-reduce(f32[8,512]{1,0:T(8,128)S(1)} %fusion.106), channel_id=1, replica_groups=mesh['row'=8,'col'=4] {'row','col'}, use_global_device_ids=true, to_apply=%region_2.2 | all-reduce | flops 4096 | bytes 32768 | tf_op jit(solution)/shard_map/while/body/eval_jaxpr/psum | solution.py:65
  53.7 1.8 fusion.106
  55.5 40.2 %psum.32 = f32[8,512]{1,0:T(8,128)S(1)} all-reduce(f32[8,512]{1,0:T(8,128)S(1)} %fusion.106), channel_id=1, replica_groups=mesh['row'=8,'col'=4] {'row','col'}, use_global_device_ids=true, to_apply=%region_2.2 | all-reduce | flops 4096 | bytes 32768 | tf_op jit(solution)/shard_map/while/body/eval_jaxpr/psum | solution.py:65
  100.2 40.0 %psum.32 = f32[8,512]{1,0:T(8,128)S(1)} all-reduce(f32[8,512]{1,0:T(8,128)S(1)} %fusion.106), channel_id=1, replica_groups=mesh['row'=8,'col'=4] {'row','col'}, use_global_device_ids=true, to_apply=%region_2.2 | all-reduce | flops 4096 | bytes 32768 | tf_op jit(solution)/shard_map/while/body/eval_jaxpr/psum | solution.py:65
  144.7 40.2 %psum.32 = f32[8,512]{1,0:T(8,128)S(1)} all-reduce(f32[8,512]{1,0:T(8,128)S(1)} %fusion.106), channel_id=1, replica_groups=mesh['row'=8,'col'=4] {'row','col'}, use_global_device_ids=true, to_apply=%region_2.2 | all-reduce | flops 4096 | bytes 32768 | tf_op jit(solution)/shard_map/while/body/eval_jaxpr/psum | solution.py:65
  187.6 1.8 fusion.106
  189.4 39.9 %psum.32 = f32[8,512]{1,0:T(8,128)S(1)} all-reduce(f32[8,512]{1,0:T(8,128)S(1)} %fusion.106), channel_id=1, replica_groups=mesh['row'=8,'col'=4] {'row','col'}, use_global_device_ids=true, to_apply=%region_2.2 | all-reduce | flops 4096 | bytes 32768 | tf_op jit(solution)/shard_map/while/body/eval_jaxpr/psum | solution.py:65
  232.0 1.8 fusion.106
  233.8 40.1 %psum.32 = f32[8,512]{1,0:T(8,128)S(1)} all-reduce(f32[8,512]{1,0:T(8,128)S(1)} %fusion.106), channel_id=1, replica_groups=mesh['row'=8,'col'=4] {'row','col'}, use_global_device_ids=true, to_apply=%region_2.2 | all-reduce | flops 4096 | bytes 32768 | tf_op jit(solution)/shard_map/while/body/eval_jaxpr/psum | solution.py:65
  276.7 1.8 fusion.106
  278.5 40.0 %psum.32 = f32[8,512]{1,0:T(8,128)S(1)} all-reduce(f32[8,512]{1,0:T(8,128)S(1)} %fusion.106), channel_id=1, replica_groups=mesh['row'=8,'col'=4] {'row','col'}, use_global_device_ids=true, to_apply=%region_2.2 | all-reduce | flops 4096 | bytes 32768 | tf_op jit(solution)/shard_map/while/body/eval_jaxpr/psum | solution.py:65
  321.2 1.8 fusion.106
  323.0 40.2 %psum.32 = f32[8,512]{1,0:T(8,128)S(1)} all-reduce(f32[8,512]{1,0:T(8,128)S(1)} %fusion.106), channel_id=1, replica_groups=mesh['row'=8,'col'=4] {'row','col'}, use_global_device_ids=true, to_apply=%region_2.2 | all-reduce | flops 4096 | bytes 32768 | tf_op jit(solution)/shard_map/while/body/eval_jaxpr/psum | solution.py:65
  365.9 1.8 fusion.106
  367.7 39.8 %psum.32 = f32[8,512]{1,0:T(8,128)S(1)} all-reduce(f32[8,512]{1,0:T(8,128)S(1)} %fusion.106), channel_id=1, replica_groups=mesh['row'=8,'col'=4] {'row','col'}, use_global_device_ids=true, to_apply=%region_2.2 | all-reduce | flops 4096 | bytes 32768 | tf_op jit(solution)/shard_map/while/body/eval_jaxpr/psum | solution.py:65
  410.2 1.8 fusion.106
  412.0 40.2 %psum.32 = f32[8,512]{1,0:T(8,128)S(1)} all-reduce(f32[8,512]{1,0:T(8,128)S(1)} %fusion.106), channel_id=1, replica_groups=mesh['row'=8,'col'=4] {'row','col'}, use_global_device_ids=true, to_apply=%region_2.2 | all-reduce | flops 4096 | bytes 32768 | tf_op jit(solution)/shard_map/while/body/eval_jaxpr/psum | solution.py:65
  455.0 1.8 fusion.106
  456.7 39.8 %psum.32 = f32[8,512]{1,0:T(8,128)S(1)} all-reduce(f32[8,512]{1,0:T(8,128)S(1)} %fusion.106), channel_id=1, replica_groups=mesh['row'=8,'col'=4] {'row','col'}, use_global_device_ids=true, to_apply=%region_2.2 | all-reduce | flops 4096 | bytes 32768 | tf_op jit(solution)/shard_map/while/body/eval_jaxpr/psum | solution.py:65
  499.3 1.8 fusion.106
  501.1 40.2 %psum.32 = f32[8,512]{1,0:T(8,128)S(1)} all-reduce(f32[8,512]{1,0:T(8,128)S(1)} %fusion.106), channel_id=1, replica_groups=mesh['row'=8,'col'=4] {'row','col'}, use_global_device_ids=true, to_apply=%region_2.2 | all-reduce | flops 4096 | bytes 32768 | tf_op jit(solution)/shard_map/while/body/eval_jaxpr/psum | solution.py:65
  544.0 1.8 fusion.106
  545.8 39.8 %psum.32 = f32[8,512]{1,0:T(8,128)S(1)} all-reduce(f32[8,512]{1,0:T(8,128)S(1)} %fusion.106), channel_id=1, replica_groups=mesh['row'=8,'col'=4] {'row','col'}, use_global_device_ids=true, to_apply=%region_2.2 | all-reduce | flops 4096 | bytes 32768 | tf_op jit(solution)/shard_map/while/body/eval_jaxpr/psum | solution.py:65
  588.3 1.8 fusion.106
  590.1 40.3 %psum.32 = f32[8,512]{1,0:T(8,128)S(1)} all-reduce(f32[8,512]{1,0:T(8,128)S(1)} %fusion.106), channel_id=1, replica_groups=mesh['row'=8,'col'=4] {'row','col'}, use_global_device_ids=true, to_apply=%region_2.2 | all-reduce | flops 4096 | bytes 32768 | tf_op jit(solution)/shard_map/while/body/eval_jaxpr/psum | solution.py:65
  633.2 1.8 fusion.106
  635.0 39.7 %psum.32 = f32[8,512]{1,0:T(8,128)S(1)} all-reduce(f32[8,512]{1,0:T(8,128)S(1)} %fusion.106), channel_id=1, replica_groups=mesh['row'=8,'col'=4] {'row','col'}, use_global_device_ids=true, to_apply=%region_2.2 | all-reduce | flops 4096 | bytes 32768 | tf_op jit(solution)/shard_map/while/body/eval_jaxpr/psum | solution.py:65
  677.4 1.8 fusion.106
  679.2 40.4 %psum.32 = f32[8,512]{1,0:T(8,128)S(1)} all-reduce(f32[8,512]{1,0:T(8,128)S(1)} %fusion.106), channel_id=1, replica_groups=mesh['row'=8,'col'=4] {'row','col'}, use_global_device_ids=true, to_apply=%region_2.2 | all-reduce | flops 4096 | bytes 32768 | tf_op jit(solution)/shard_map/while/body/eval_jaxpr/psum | solution.py:65
  721.8 700.1 %while.33 = (s32[]{:T(128)}, f32[8,16,512]{2,0,1:T(8,128)S(1)}, f32[8,16,512]{2,0,1:T(8,128)S(1)}, s32[2,4]{0,1:T(4,128)S(1)}, s32[]{:T(128)}, /*index=5*/bf16[2...) while((s32[]{:T(128)}, f32[8,16,512]{2,0,1:T(8,128)S(1)}, ...), condition=%wide.region_6.7_spmd.clone, body=%wide.region_4.6_spmd.clone.sunk | while | flops 29382456 | bytes 1203697 | solution.py:99
  724.0 39.6 %psum.33 = f32[8,512]{1,0:T(8,128)S(1)} all-reduce(f32[8,512]{1,0:T(8,128)S(1)} %fusion.113), channel_id=1, replica_groups=mesh['row'=8,'col'=4] {'row','col'}, use_global_device_ids=true, to_apply=%region_5.5 | all-reduce | flops 4096 | bytes 32768 | tf_op jit(solution)/shard_map/while/body/eval_jaxpr/psum | solution.py:93
  767.2 40.5 %psum.33 = f32[8,512]{1,0:T(8,128)S(1)} all-reduce(f32[8,512]{1,0:T(8,128)S(1)} %fusion.113), channel_id=1, replica_groups=mesh['row'=8,'col'=4] {'row','col'}, use_global_device_ids=true, to_apply=%region_5.5 | all-reduce | flops 4096 | bytes 32768 | tf_op jit(solution)/shard_map/while/body/eval_jaxpr/psum | solution.py:93
  811.5 39.5 %psum.33 = f32[8,512]{1,0:T(8,128)S(1)} all-reduce(f32[8,512]{1,0:T(8,128)S(1)} %fusion.113), channel_id=1, replica_groups=mesh['row'=8,'col'=4] {'row','col'}, use_global_device_ids=true, to_apply=%region_5.5 | all-reduce | flops 4096 | bytes 32768 | tf_op jit(solution)/shard_map/while/body/eval_jaxpr/psum | solution.py:93
  854.7 40.6 %psum.33 = f32[8,512]{1,0:T(8,128)S(1)} all-reduce(f32[8,512]{1,0:T(8,128)S(1)} %fusion.113), channel_id=1, replica_groups=mesh['row'=8,'col'=4] {'row','col'}, use_global_device_ids=true, to_apply=%region_5.5 | all-reduce | flops 4096 | bytes 32768 | tf_op jit(solution)/shard_map/while/body/eval_jaxpr/psum | solution.py:93
  899.0 39.4 %psum.33 = f32[8,512]{1,0:T(8,128)S(1)} all-reduce(f32[8,512]{1,0:T(8,128)S(1)} %fusion.113), channel_id=1, replica_groups=mesh['row'=8,'col'=4] {'row','col'}, use_global_device_ids=true, to_apply=%region_5.5 | all-reduce | flops 4096 | bytes 32768 | tf_op jit(solution)/shard_map/while/body/eval_jaxpr/psum | solution.py:93
  942.1 40.7 %psum.33 = f32[8,512]{1,0:T(8,128)S(1)} all-reduce(f32[8,512]{1,0:T(8,128)S(1)} %fusion.113), channel_id=1, replica_groups=mesh['row'=8,'col'=4] {'row','col'}, use_global_device_ids=true, to_apply=%region_5.5 | all-reduce | flops 4096 | bytes 32768 | tf_op jit(solution)/shard_map/while/body/eval_jaxpr/psum | solution.py:93
  986.5 39.4 %psum.33 = f32[8,512]{1,0:T(8,128)S(1)} all-reduce(f32[8,512]{1,0:T(8,128)S(1)} %fusion.113), channel_id=1, replica_groups=mesh['row'=8,'col'=4] {'row','col'}, use_global_device_ids=true, to_apply=%region_5.5 | all-reduce | flops 4096 | bytes 32768 | tf_op jit(solution)/shard_map/while/body/eval_jaxpr/psum | solution.py:93
  1029.6 40.7 %psum.33 = f32[8,512]{1,0:T(8,128)S(1)} all-reduce(f32[8,512]{1,0:T(8,128)S(1)} %fusion.113), channel_id=1, replica_groups=mesh['row'=8,'col'=4] {'row','col'}, use_global_device_ids=true, to_apply=%region_5.5 | all-reduce | flops 4096 | bytes 32768 | tf_op jit(solution)/shard_map/while/body/eval_jaxpr/psum | solution.py:93
  1074.0 39.4 %psum.33 = f32[8,512]{1,0:T(8,128)S(1)} all-reduce(f32[8,512]{1,0:T(8,128)S(1)} %fusion.113), channel_id=1, replica_groups=mesh['row'=8,'col'=4] {'row','col'}, use_global_device_ids=true, to_apply=%region_5.5 | all-reduce | flops 4096 | bytes 32768 | tf_op jit(solution)/shard_map/while/body/eval_jaxpr/psum | solution.py:93
  1117.1 40.7 %psum.33 = f32[8,512]{1,0:T(8,128)S(1)} all-reduce(f32[8,512]{1,0:T(8,128)S(1)} %fusion.113), channel_id=1, replica_groups=mesh['row'=8,'col'=4] {'row','col'}, use_global_device_ids=true, to_apply=%region_5.5 | all-reduce | flops 4096 | bytes 32768 | tf_op jit(solution)/shard_map/while/body/eval_jaxpr/psum | solution.py:93
  1161.5 39.4 %psum.33 = f32[8,512]{1,0:T(8,128)S(1)} all-reduce(f32[8,512]{1,0:T(8,128)S(1)} %fusion.113), channel_id=1, replica_groups=mesh['row'=8,'col'=4] {'row','col'}, use_global_device_ids=true, to_apply=%region_5.5 | all-reduce | flops 4096 | bytes 32768 | tf_op jit(solution)/shard_map/while/body/eval_jaxpr/psum | solution.py:93
  1204.6 40.7 %psum.33 = f32[8,512]{1,0:T(8,128)S(1)} all-reduce(f32[8,512]{1,0:T(8,128)S(1)} %fusion.113), channel_id=1, replica_groups=mesh['row'=8,'col'=4] {'row','col'}, use_global_device_ids=true, to_apply=%region_5.5 | all-reduce | flops 4096 | bytes 32768 | tf_op jit(solution)/shard_map/while/body/eval_jaxpr/psum | solution.py:93
  1249.0 39.4 %psum.33 = f32[8,512]{1,0:T(8,128)S(1)} all-reduce(f32[8,512]{1,0:T(8,128)S(1)} %fusion.113), channel_id=1, replica_groups=mesh['row'=8,'col'=4] {'row','col'}, use_global_device_ids=true, to_apply=%region_5.5 | all-reduce | flops 4096 | bytes 32768 | tf_op jit(solution)/shard_map/while/body/eval_jaxpr/psum | solution.py:93
  1292.2 40.7 %psum.33 = f32[8,512]{1,0:T(8,128)S(1)} all-reduce(f32[8,512]{1,0:T(8,128)S(1)} %fusion.113), channel_id=1, replica_groups=mesh['row'=8,'col'=4] {'row','col'}, use_global_device_ids=true, to_apply=%region_5.5 | all-reduce | flops 4096 | bytes 32768 | tf_op jit(solution)/shard_map/while/body/eval_jaxpr/psum | solution.py:93
  1336.5 39.4 %psum.33 = f32[8,512]{1,0:T(8,128)S(1)} all-reduce(f32[8,512]{1,0:T(8,128)S(1)} %fusion.113), channel_id=1, replica_groups=mesh['row'=8,'col'=4] {'row','col'}, use_global_device_ids=true, to_apply=%region_5.5 | all-reduce | flops 4096 | bytes 32768 | tf_op jit(solution)/shard_map/while/body/eval_jaxpr/psum | solution.py:93
  1379.7 40.7 %psum.33 = f32[8,512]{1,0:T(8,128)S(1)} all-reduce(f32[8,512]{1,0:T(8,128)S(1)} %fusion.113), channel_id=1, replica_groups=mesh['row'=8,'col'=4] {'row','col'}, use_global_device_ids=true, to_apply=%region_5.5 | all-reduce | flops 4096 | bytes 32768 | tf_op jit(solution)/shard_map/while/body/eval_jaxpr/psum | solution.py:93
  (262 shorter events, 113.8 us)
Async XLA Ops:
  0.6 1422.8 %copy-start = (bf16[1,512,512]{2,1,0:T(8,128)(2,1)S(1)}, bf16[1,512,512]{2,1,0:T(8,128)(2,1)}, u32[]{:S(2)}) copy-start(bf16[1,512,512]{2,1,0:T(8,128)(2,1)} %param.20) | copy-start | bytes 1572868
  5.7 1417.3 %copy-start.1 = (bf16[1,512,1024]{2,1,0:T(8,128)(2,1)S(1)}, bf16[1,512,1024]{2,1,0:T(8,128)(2,1)}, u32[]{:S(2)}) copy-start(bf16[1,512,1024]{2,1,0:T(8,128)(2,1)} %param.19) | copy-start | bytes 3145732
  5.8 1417.7 %copy-start.2 = (bf16[1,8,512]{2,1,0:T(8,128)(2,1)S(1)}, bf16[1,8,512]{2,1,0:T(8,128)(2,1)}, u32[]{:S(2)}) copy-start(bf16[1,8,512]{2,1,0:T(8,128)(2,1)} %param.18) | copy-start | bytes 24580
where the time goes:
time: 1430 us; the launch traced here: 1420 us
  blocking collectives  1280 us (90%)
  matrix products  100 us (7%)
  local copies, waits for them, and re-layouts  33.4 us (2%)
    psum x16, blocking collectives, forward(): row_total = lax.psum(partial_value + carried, ('row', 'col'))  643 us
    psum x16, blocking collectives, backward(): col_total = lax.psum(partial_value, ('row', 'col'))  641 us

commit v1 on v0

--- a/solution.py
+++ b/solution.py
@@ -90,7 +90,7 @@
         partial_value = jnp.einsum(
             "raq,atq->rt", coefficient_values, right_col, preferred_element_type=jnp.float32
         )
-        col_total = lax.psum(partial_value, ("row", "col"))
+        col_total = jnp.sum(lax.all_gather(partial_value, ("row", "col")), axis=0)
         block_solved = lax.dynamic_index_in_dim(solved_rows, column, 1, keepdims=False)
         inverse = lax.dynamic_index_in_dim(diag_inv, column, 0, keepdims=False).astype(jnp.float32)
         fresh = jnp.dot(block_solved - col_total, inverse.T, precision=highest_precision)

time: 1430 us -> 1410 us (0.986)
    psum x16 -> x0, blocking collectives: 641 us -> none  [backward(): col_total = lax.psum(partial_value, ('row', 'col'))]
    all_gather x0 -> x16, blocking collectives: none -> 623 us  [backward(): col_total = jnp.sum(lax.all_gather(partial_value, ('row', 'col')), axis=0)]
where the time goes in v1:
time: 1410 us
  blocking collectives  1270 us (90%)
  matrix products  97.7 us (7%)
  local copies, waits for them, and re-layouts  34.8 us (2%)
    psum x16, blocking collectives, forward(): row_total = lax.psum(partial_value + carried, ('row', 'col'))  643 us
    all_gather x16, blocking collectives, backward(): col_total = jnp.sum(lax.all_gather(partial_value, ('row', 'col')), axis=0)  623 us
    dot_general x16, matrix products, forward(): jnp.einsum('rbq,bqt->rt', coefficient_values, left_row_index, preferred_e...  28.5 us

profile of v1, /device:TPU:0, one launch (start us, length us, event | category | flops | bytes accessed | tf_op | source)
XLA Modules:
  0.0 1406.6 jit_solution(297303613746316633)
XLA Ops:
  5.7 715.3 %while.32 = (s32[]{:T(128)}, f32[8,16,512]{2,0,1:T(8,128)S(1)}, bf16[8,16,512]{2,1,0:T(8,128)(2,1)S(1)}, s32[2,4]{1,0:T(2,128)}, s32[]{:T(128)}, /*index=5*/bf16...) while((s32[]{:T(128)}, f32[8,16,512]{2,0,1:T(8,128)S(1)}, ...), condition=%wide.region_3.4_spmd.clone, body=%wide.region_1.3_spmd.clone.sunk | while | flops 33598024 | bytes 1818560 | solution.py:73
  7.1 1.8 fusion.105
  8.9 42.0 %psum.16 = f32[8,512]{1,0:T(8,128)S(1)} all-reduce(f32[8,512]{1,0:T(8,128)S(1)} %fusion.105), channel_id=1, replica_groups=mesh['row'=8,'col'=4] {'row','col'}, use_global_device_ids=true, to_apply=%region_2.2 | all-reduce | flops 4096 | bytes 32768 | tf_op jit(solution)/shard_map/while/body/eval_jaxpr/psum | solution.py:65
  53.6 1.8 fusion.105
  55.4 40.2 %psum.16 = f32[8,512]{1,0:T(8,128)S(1)} all-reduce(f32[8,512]{1,0:T(8,128)S(1)} %fusion.105), channel_id=1, replica_groups=mesh['row'=8,'col'=4] {'row','col'}, use_global_device_ids=true, to_apply=%region_2.2 | all-reduce | flops 4096 | bytes 32768 | tf_op jit(solution)/shard_map/while/body/eval_jaxpr/psum | solution.py:65
  98.3 1.8 fusion.105
  100.1 40.0 %psum.16 = f32[8,512]{1,0:T(8,128)S(1)} all-reduce(f32[8,512]{1,0:T(8,128)S(1)} %fusion.105), channel_id=1, replica_groups=mesh['row'=8,'col'=4] {'row','col'}, use_global_device_ids=true, to_apply=%region_2.2 | all-reduce | flops 4096 | bytes 32768 | tf_op jit(solution)/shard_map/while/body/eval_jaxpr/psum | solution.py:65
  142.8 1.8 fusion.105
  144.6 40.2 %psum.16 = f32[8,512]{1,0:T(8,128)S(1)} all-reduce(f32[8,512]{1,0:T(8,128)S(1)} %fusion.105), channel_id=1, replica_groups=mesh['row'=8,'col'=4] {'row','col'}, use_global_device_ids=true, to_apply=%region_2.2 | all-reduce | flops 4096 | bytes 32768 | tf_op jit(solution)/shard_map/while/body/eval_jaxpr/psum | solution.py:65
  187.5 1.8 fusion.105
  189.3 39.9 %psum.16 = f32[8,512]{1,0:T(8,128)S(1)} all-reduce(f32[8,512]{1,0:T(8,128)S(1)} %fusion.105), channel_id=1, replica_groups=mesh['row'=8,'col'=4] {'row','col'}, use_global_device_ids=true, to_apply=%region_2.2 | all-reduce | flops 4096 | bytes 32768 | tf_op jit(solution)/shard_map/while/body/eval_jaxpr/psum | solution.py:65
  231.9 1.8 fusion.105
  233.7 40.1 %psum.16 = f32[8,512]{1,0:T(8,128)S(1)} all-reduce(f32[8,512]{1,0:T(8,128)S(1)} %fusion.105), channel_id=1, replica_groups=mesh['row'=8,'col'=4] {'row','col'}, use_global_device_ids=true, to_apply=%region_2.2 | all-reduce | flops 4096 | bytes 32768 | tf_op jit(solution)/shard_map/while/body/eval_jaxpr/psum | solution.py:65
  278.4 39.9 %psum.16 = f32[8,512]{1,0:T(8,128)S(1)} all-reduce(f32[8,512]{1,0:T(8,128)S(1)} %fusion.105), channel_id=1, replica_groups=mesh['row'=8,'col'=4] {'row','col'}, use_global_device_ids=true, to_apply=%region_2.2 | all-reduce | flops 4096 | bytes 32768 | tf_op jit(solution)/shard_map/while/body/eval_jaxpr/psum | solution.py:65
  321.0 1.8 fusion.105
  322.8 40.2 %psum.16 = f32[8,512]{1,0:T(8,128)S(1)} all-reduce(f32[8,512]{1,0:T(8,128)S(1)} %fusion.105), channel_id=1, replica_groups=mesh['row'=8,'col'=4] {'row','col'}, use_global_device_ids=true, to_apply=%region_2.2 | all-reduce | flops 4096 | bytes 32768 | tf_op jit(solution)/shard_map/while/body/eval_jaxpr/psum | solution.py:65
  367.6 39.8 %psum.16 = f32[8,512]{1,0:T(8,128)S(1)} all-reduce(f32[8,512]{1,0:T(8,128)S(1)} %fusion.105), channel_id=1, replica_groups=mesh['row'=8,'col'=4] {'row','col'}, use_global_device_ids=true, to_apply=%region_2.2 | all-reduce | flops 4096 | bytes 32768 | tf_op jit(solution)/shard_map/while/body/eval_jaxpr/psum | solution.py:65
  410.1 1.8 fusion.105
  411.9 40.2 %psum.16 = f32[8,512]{1,0:T(8,128)S(1)} all-reduce(f32[8,512]{1,0:T(8,128)S(1)} %fusion.105), channel_id=1, replica_groups=mesh['row'=8,'col'=4] {'row','col'}, use_global_device_ids=true, to_apply=%region_2.2 | all-reduce | flops 4096 | bytes 32768 | tf_op jit(solution)/shard_map/while/body/eval_jaxpr/psum | solution.py:65
  454.9 1.8 fusion.105
  456.7 39.8 %psum.16 = f32[8,512]{1,0:T(8,128)S(1)} all-reduce(f32[8,512]{1,0:T(8,128)S(1)} %fusion.105), channel_id=1, replica_groups=mesh['row'=8,'col'=4] {'row','col'}, use_global_device_ids=true, to_apply=%region_2.2 | all-reduce | flops 4096 | bytes 32768 | tf_op jit(solution)/shard_map/while/body/eval_jaxpr/psum | solution.py:65
  499.2 1.8 fusion.105
  501.0 40.4 %psum.16 = f32[8,512]{1,0:T(8,128)S(1)} all-reduce(f32[8,512]{1,0:T(8,128)S(1)} %fusion.105), channel_id=1, replica_groups=mesh['row'=8,'col'=4] {'row','col'}, use_global_device_ids=true, to_apply=%region_2.2 | all-reduce | flops 4096 | bytes 32768 | tf_op jit(solution)/shard_map/while/body/eval_jaxpr/psum | solution.py:65
  544.1 1.8 fusion.105
  545.9 39.7 %psum.16 = f32[8,512]{1,0:T(8,128)S(1)} all-reduce(f32[8,512]{1,0:T(8,128)S(1)} %fusion.105), channel_id=1, replica_groups=mesh['row'=8,'col'=4] {'row','col'}, use_global_device_ids=true, to_apply=%region_2.2 | all-reduce | flops 4096 | bytes 32768 | tf_op jit(solution)/shard_map/while/body/eval_jaxpr/psum | solution.py:65
  588.3 1.8 fusion.105
  590.0 40.4 %psum.16 = f32[8,512]{1,0:T(8,128)S(1)} all-reduce(f32[8,512]{1,0:T(8,128)S(1)} %fusion.105), channel_id=1, replica_groups=mesh['row'=8,'col'=4] {'row','col'}, use_global_device_ids=true, to_apply=%region_2.2 | all-reduce | flops 4096 | bytes 32768 | tf_op jit(solution)/shard_map/while/body/eval_jaxpr/psum | solution.py:65
  633.2 1.8 fusion.105
  635.0 39.6 %psum.16 = f32[8,512]{1,0:T(8,128)S(1)} all-reduce(f32[8,512]{1,0:T(8,128)S(1)} %fusion.105), channel_id=1, replica_groups=mesh['row'=8,'col'=4] {'row','col'}, use_global_device_ids=true, to_apply=%region_2.2 | all-reduce | flops 4096 | bytes 32768 | tf_op jit(solution)/shard_map/while/body/eval_jaxpr/psum | solution.py:65
  677.3 1.8 fusion.105
  679.1 40.5 %psum.16 = f32[8,512]{1,0:T(8,128)S(1)} all-reduce(f32[8,512]{1,0:T(8,128)S(1)} %fusion.105), channel_id=1, replica_groups=mesh['row'=8,'col'=4] {'row','col'}, use_global_device_ids=true, to_apply=%region_2.2 | all-reduce | flops 4096 | bytes 32768 | tf_op jit(solution)/shard_map/while/body/eval_jaxpr/psum | solution.py:65
  723.2 680.9 %while.33 = (s32[]{:T(128)}, f32[8,16,512]{2,0,1:T(8,128)S(1)}, f32[8,16,512]{2,0,1:T(8,128)S(1)}, s32[2,4]{0,1:T(4,128)S(1)}, s32[]{:T(128)}, /*index=5*/bf16[2...) while((s32[]{:T(128)}, f32[8,16,512]{2,0,1:T(8,128)S(1)}, ...), condition=%wide.region_6.7_spmd.clone, body=%wide.region_4.6_spmd.clone.sunk | while | flops 29505336 | bytes 2318067 | solution.py:99
  725.2 42.6 %all-gather.3 = f32[256,512]{1,0:T(8,128)S(1)} all-gather(f32[8,512]{1,0:T(8,128)S(1)} %convolution_bitcast_fusion.6), channel_id=2, replica_groups=mesh['row'=8,'col'=4] {'row','col'}, dimensions={0}, use_global_device_ids=true | all-gather | bytes 540672 | tf_op jit(solution)/shard_map/while/body/eval_jaxpr/all_gather | solution.py:93
  771.4 38.1 %all-gather.3 = f32[256,512]{1,0:T(8,128)S(1)} all-gather(f32[8,512]{1,0:T(8,128)S(1)} %convolution_bitcast_fusion.6), channel_id=2, replica_groups=mesh['row'=8,'col'=4] {'row','col'}, dimensions={0}, use_global_device_ids=true | all-gather | bytes 540672 | tf_op jit(solution)/shard_map/while/body/eval_jaxpr/all_gather | solution.py:93
  813.0 39.4 %all-gather.3 = f32[256,512]{1,0:T(8,128)S(1)} all-gather(f32[8,512]{1,0:T(8,128)S(1)} %convolution_bitcast_fusion.6), channel_id=2, replica_groups=mesh['row'=8,'col'=4] {'row','col'}, dimensions={0}, use_global_device_ids=true | all-gather | bytes 540672 | tf_op jit(solution)/shard_map/while/body/eval_jaxpr/all_gather | solution.py:93
  856.1 38.1 %all-gather.3 = f32[256,512]{1,0:T(8,128)S(1)} all-gather(f32[8,512]{1,0:T(8,128)S(1)} %convolution_bitcast_fusion.6), channel_id=2, replica_groups=mesh['row'=8,'col'=4] {'row','col'}, dimensions={0}, use_global_device_ids=true | all-gather | bytes 540672 | tf_op jit(solution)/shard_map/while/body/eval_jaxpr/all_gather | solution.py:93
  897.8 39.4 %all-gather.3 = f32[256,512]{1,0:T(8,128)S(1)} all-gather(f32[8,512]{1,0:T(8,128)S(1)} %convolution_bitcast_fusion.6), channel_id=2, replica_groups=mesh['row'=8,'col'=4] {'row','col'}, dimensions={0}, use_global_device_ids=true | all-gather | bytes 540672 | tf_op jit(solution)/shard_map/while/body/eval_jaxpr/all_gather | solution.py:93
  940.8 38.1 %all-gather.3 = f32[256,512]{1,0:T(8,128)S(1)} all-gather(f32[8,512]{1,0:T(8,128)S(1)} %convolution_bitcast_fusion.6), channel_id=2, replica_groups=mesh['row'=8,'col'=4] {'row','col'}, dimensions={0}, use_global_device_ids=true | all-gather | bytes 540672 | tf_op jit(solution)/shard_map/while/body/eval_jaxpr/all_gather | solution.py:93
  982.5 39.4 %all-gather.3 = f32[256,512]{1,0:T(8,128)S(1)} all-gather(f32[8,512]{1,0:T(8,128)S(1)} %convolution_bitcast_fusion.6), channel_id=2, replica_groups=mesh['row'=8,'col'=4] {'row','col'}, dimensions={0}, use_global_device_ids=true | all-gather | bytes 540672 | tf_op jit(solution)/shard_map/while/body/eval_jaxpr/all_gather | solution.py:93
  1025.5 38.1 %all-gather.3 = f32[256,512]{1,0:T(8,128)S(1)} all-gather(f32[8,512]{1,0:T(8,128)S(1)} %convolution_bitcast_fusion.6), channel_id=2, replica_groups=mesh['row'=8,'col'=4] {'row','col'}, dimensions={0}, use_global_device_ids=true | all-gather | bytes 540672 | tf_op jit(solution)/shard_map/while/body/eval_jaxpr/all_gather | solution.py:93
  1067.2 39.4 %all-gather.3 = f32[256,512]{1,0:T(8,128)S(1)} all-gather(f32[8,512]{1,0:T(8,128)S(1)} %convolution_bitcast_fusion.6), channel_id=2, replica_groups=mesh['row'=8,'col'=4] {'row','col'}, dimensions={0}, use_global_device_ids=true | all-gather | bytes 540672 | tf_op jit(solution)/shard_map/while/body/eval_jaxpr/all_gather | solution.py:93
  1110.2 38.1 %all-gather.3 = f32[256,512]{1,0:T(8,128)S(1)} all-gather(f32[8,512]{1,0:T(8,128)S(1)} %convolution_bitcast_fusion.6), channel_id=2, replica_groups=mesh['row'=8,'col'=4] {'row','col'}, dimensions={0}, use_global_device_ids=true | all-gather | bytes 540672 | tf_op jit(solution)/shard_map/while/body/eval_jaxpr/all_gather | solution.py:93
  1151.9 39.4 %all-gather.3 = f32[256,512]{1,0:T(8,128)S(1)} all-gather(f32[8,512]{1,0:T(8,128)S(1)} %convolution_bitcast_fusion.6), channel_id=2, replica_groups=mesh['row'=8,'col'=4] {'row','col'}, dimensions={0}, use_global_device_ids=true | all-gather | bytes 540672 | tf_op jit(solution)/shard_map/while/body/eval_jaxpr/all_gather | solution.py:93
  1194.9 38.1 %all-gather.3 = f32[256,512]{1,0:T(8,128)S(1)} all-gather(f32[8,512]{1,0:T(8,128)S(1)} %convolution_bitcast_fusion.6), channel_id=2, replica_groups=mesh['row'=8,'col'=4] {'row','col'}, dimensions={0}, use_global_device_ids=true | all-gather | bytes 540672 | tf_op jit(solution)/shard_map/while/body/eval_jaxpr/all_gather | solution.py:93
  1236.6 39.4 %all-gather.3 = f32[256,512]{1,0:T(8,128)S(1)} all-gather(f32[8,512]{1,0:T(8,128)S(1)} %convolution_bitcast_fusion.6), channel_id=2, replica_groups=mesh['row'=8,'col'=4] {'row','col'}, dimensions={0}, use_global_device_ids=true | all-gather | bytes 540672 | tf_op jit(solution)/shard_map/while/body/eval_jaxpr/all_gather | solution.py:93
  1279.6 38.1 %all-gather.3 = f32[256,512]{1,0:T(8,128)S(1)} all-gather(f32[8,512]{1,0:T(8,128)S(1)} %convolution_bitcast_fusion.6), channel_id=2, replica_groups=mesh['row'=8,'col'=4] {'row','col'}, dimensions={0}, use_global_device_ids=true | all-gather | bytes 540672 | tf_op jit(solution)/shard_map/while/body/eval_jaxpr/all_gather | solution.py:93
  1321.3 39.4 %all-gather.3 = f32[256,512]{1,0:T(8,128)S(1)} all-gather(f32[8,512]{1,0:T(8,128)S(1)} %convolution_bitcast_fusion.6), channel_id=2, replica_groups=mesh['row'=8,'col'=4] {'row','col'}, dimensions={0}, use_global_device_ids=true | all-gather | bytes 540672 | tf_op jit(solution)/shard_map/while/body/eval_jaxpr/all_gather | solution.py:93
  1364.4 38.1 %all-gather.3 = f32[256,512]{1,0:T(8,128)S(1)} all-gather(f32[8,512]{1,0:T(8,128)S(1)} %convolution_bitcast_fusion.6), channel_id=2, replica_groups=mesh['row'=8,'col'=4] {'row','col'}, dimensions={0}, use_global_device_ids=true | all-gather | bytes 540672 | tf_op jit(solution)/shard_map/while/body/eval_jaxpr/all_gather | solution.py:93
  (311 shorter events, 113.8 us)
Async XLA Ops:
  0.6 1405.0 %copy-start = (bf16[1,512,512]{2,1,0:T(8,128)(2,1)S(1)}, bf16[1,512,512]{2,1,0:T(8,128)(2,1)}, u32[]{:S(2)}) copy-start(bf16[1,512,512]{2,1,0:T(8,128)(2,1)} %param.20) | copy-start | bytes 1572868
  721.0 684.2 %copy-start.1 = (bf16[1,512,1024]{2,1,0:T(8,128)(2,1)S(1)}, bf16[1,512,1024]{2,1,0:T(8,128)(2,1)}, u32[]{:S(2)}) copy-start(bf16[1,512,1024]{2,1,0:T(8,128)(2,1)} %param.19) | copy-start | bytes 3145732
  721.0 684.6 %copy-start.2 = (bf16[1,8,512]{2,1,0:T(8,128)(2,1)S(1)}, bf16[1,8,512]{2,1,0:T(8,128)(2,1)}, u32[]{:S(2)}) copy-start(bf16[1,8,512]{2,1,0:T(8,128)(2,1)} %param.18) | copy-start | bytes 24580
